TPU v7x, 128 devices: a whole 4x4x4 slice. The times are simulated.
128 devices in a mesh: cell: 8 (over z, core), tm: 16 (over y, x).
Axes of the slice: x: 4, y: 4, z: 4, core: 2. Of those that a mesh axis runs over, the one named last changes fastest.
Arguments:
- solution: float32 [32768], P(('cell', 'tm')), may hold values from -6 to 6
- residual: float32 [32768], P(('cell', 'tm')), may hold values from -8 to 8
- direction: float32 [32768], P(('cell', 'tm')), may hold values from -8 to 8
- noise_var: float32 [32768], P(('cell', 'tm')), may hold values from 0.5 to 2
- footprints: bfloat16 [262144, 128], P(('cell', 'tm')), may hold values from -0.5 to 0.5
- tile_owner: int32 [262144, 1], P(('cell', 'tm')), may hold values from 0 to 127; in each aligned block of 2048 rows (0 to 2047, 2048 to 4095, ...) at most 32 rows name the same one
- tile_block: int32 [262144], P(('cell', 'tm')), may hold values from 0 to 8
- tile_step: int32 [262144], P(('cell', 'tm')), may hold values from 0 to 127
- tile_obs: int32 [262144], P(('cell', 'tm')), may hold values from 0 to 255
- cell_cov: bfloat16 [9216, 9216], P('cell'), may hold values from -2 to 7, as said below
- time_cov: bfloat16 [2048, 2048], P('tm'), may hold values from -2 to 7, as said below
Outputs:
- new_solution: float32 [32768], P(('cell', 'tm'))
- new_residual: float32 [32768], P(('cell', 'tm'))
- new_direction: float32 [32768], P(('cell', 'tm'))
Inputs may be any that keep to these rules, and one draw needn't show every extreme that they name: `tile_owner`: among the 2048 tiles of one device, no owner is named by more than 32 of them. `cell_cov`: symmetric positive definite. `time_cov`: symmetric positive definite.
All inputs are finite; a program needn't handle non-finite values.
Results may differ from a plain program's by a relative error of at most 0.0021.
Values may be sent and summed in bfloat16 or wider, within the bound.
A program may use at most 128 MiB of HBM per device.

v0:
```python
import functools
import jax
import jax.numpy as jnp
from jax import lax
from jax.sharding import Mesh
from jax.sharding import PartitionSpec as P

CELL = ("cell_0", "cell_1")
TM = ("tm_0", "tm_1")
CELL_TM = ("cell_0", "cell_1", "tm_0", "tm_1")


def laid_out(pieces, dim):
    lengths = list(pieces.shape[1:])
    lengths[dim] *= pieces.shape[0]
    return jnp.moveaxis(pieces, 0, dim).reshape(lengths)


def from_everyone(value, axis):
    peers = lax.axis_size(axis)
    return lax.all_to_all(
        jnp.broadcast_to(value[None], (peers, *value.shape)), axis, 0, 0, tiled=True
    )


def collect(value, axis, dim):
    return laid_out(from_everyone(value, axis), dim)


def over_axes(value, axes):
    return functools.reduce(lax.psum, axes, value)


def local(
    solution,
    residual,
    direction,
    noise_var,
    footprints,
    tile_owner,
    tile_block,
    tile_step,
    tile_obs,
    cell_cov,
    time_cov,
):
    devices = lax.axis_size(CELL) * lax.axis_size(TM)
    tile_count = footprints.shape[0]
    block_len = footprints.shape[1]
    cell_local = cell_cov.shape[0]
    time_local = time_cov.shape[0]
    block_local = cell_local // block_len
    obs_local = direction.shape[0]
    capacity = max(2, 2 * tile_count // devices)
    slot_total = devices * capacity
    owner_dev = tile_owner[:, 0]
    owner_hot = (owner_dev[:, None] == jnp.arange(devices, dtype=jnp.int32)[None, :]).astype(
        jnp.int32
    )
    slot_rank = jnp.sum(jnp.cumsum(owner_hot, axis=0) * owner_hot, axis=1) - 1
    slot_index = owner_dev * capacity + slot_rank
    obs_hot = (tile_obs[:, None] == jnp.arange(obs_local, dtype=jnp.int32)[None, :]).astype(
        jnp.float32
    )
    dir_tile = jnp.dot(obs_hot, direction, precision=lax.Precision.HIGHEST).astype(jnp.bfloat16)
    tile_place = tile_step * block_local + tile_block
    send_values = jnp.zeros((slot_total, block_len), jnp.bfloat16).at[slot_index].set(footprints)
    send_dir = jnp.zeros((slot_total,), jnp.bfloat16).at[slot_index].set(dir_tile)
    send_place = jnp.zeros((slot_total,), jnp.int32).at[slot_index].set(tile_place)
    got_values, got_dir, got_place = (
        lax.all_to_all(
            send_values.reshape(devices, capacity, block_len),
            CELL_TM,
            split_axis=0,
            concat_axis=0,
            tiled=True,
        ),
        lax.all_to_all(
            send_dir.reshape(devices, capacity), CELL_TM, split_axis=0, concat_axis=0, tiled=True
        ),
        lax.all_to_all(
            send_place.reshape(devices, capacity), CELL_TM, split_axis=0, concat_axis=0, tiled=True
        ),
    )
    got_values = got_values.reshape(slot_total, block_len).astype(jnp.float32)
    got_dir = got_dir.reshape(slot_total).astype(jnp.float32)
    got_place = got_place.reshape(slot_total)
    flux_time = jnp.zeros((time_local * block_local, block_len), jnp.float32)
    flux_time = flux_time.at[got_place].add(got_dir[:, None] * got_values)
    flux_grid = flux_time.reshape(time_local, cell_local).T.astype(jnp.bfloat16)
    mixed_cells = jnp.dot(
        cell_cov, collect(flux_grid, CELL, 0), preferred_element_type=jnp.float32
    ).astype(jnp.bfloat16)
    smoothed = lax.dot_general(
        time_cov,
        lax.all_gather(mixed_cells, TM, axis=1, tiled=True),
        (((1,), (1,)), ((), ())),
        preferred_element_type=jnp.float32,
    )
    smoothed = smoothed.astype(jnp.bfloat16).reshape(time_local * block_local, block_len)
    slot_dots = jnp.sum(got_values * smoothed[got_place].astype(jnp.float32), axis=1)
    returned = lax.all_to_all(
        slot_dots.reshape(devices, capacity), CELL_TM, split_axis=0, concat_axis=0, tiled=True
    )
    tile_dots = returned.reshape(slot_total)[slot_index]
    applied = jnp.dot(tile_dots, obs_hot, precision=lax.Precision.HIGHEST) + noise_var * direction
    norm_now, curvature, cross_term, image_norm = (
        over_axes(jnp.sum(residual * residual), CELL_TM),
        over_axes(jnp.sum(direction * applied), CELL_TM),
        over_axes(jnp.sum(residual * applied), CELL_TM),
        over_axes(jnp.sum(applied * applied), CELL_TM),
    )
    step_size = norm_now / curvature
    new_solution = solution + step_size * direction
    new_residual = residual - step_size * applied
    norm_next = norm_now - 2.0 * step_size * cross_term + step_size * step_size * image_norm
    new_direction = new_residual + norm_next / norm_now * direction
    return (new_solution, new_residual, new_direction)


def solution(mesh):
    finer = Mesh(mesh.devices.reshape(4, 2, 4, 4), ("cell_0", "cell_1", "tm_0", "tm_1"))
    in_specs = (
        P(CELL_TM),
        P(CELL_TM),
        P(CELL_TM),
        P(CELL_TM),
        P(CELL_TM, None),
        P(CELL_TM, None),
        P(CELL_TM),
        P(CELL_TM),
        P(CELL_TM),
        P(CELL, None),
        P(TM, None),
    )
    out_specs = (P(CELL_TM), P(CELL_TM), P(CELL_TM))
    return jax.shard_map(local, mesh=finer, in_specs=in_specs, out_specs=out_specs, check_vma=False)
```

profile of v0, /device:TPU:0, one launch (start us, length us, event | category | flops | bytes accessed | tf_op | source)
XLA Modules:
  0.0 305.8 jit_solution(9273110876222847107)
XLA Ops:
  7.2 0.9 copy.20
  8.0 0.3 fusion.8
  8.6 0.3 copy.21
  8.9 0.2 copy-done.1
  9.1 0.6 fusion.5
  9.8 1.0 fusion.4
  10.9 14.6 %scatter_custom_fusion.2 = bf16[4096]{0:T(1024)(128)(2,1)S(1)} fusion(s32[2048]{0:T(1024)S(1)} %bitcast.43, bf16[2048]{0:T(1024)(128)(2,1)S(1)} %convert_element_type.58, bf16[]{:T(256)} %constant.10.clone.1), kind=kCustom, calls=%fused_computation.39 | custom fusion | bytes 8194 | tf_op jit(solution)/shard_map/scatter | solution.py:68
  25.5 0.7 all_to_all.32
  26.2 11.2 %all-to-all-start.2 = ((bf16[128,1,32]{2,1,0:T(2,128)(2,1)}), bf16[128,1,32]{2,1,0:T(2,128)(2,1)S(1)}, u32[]{:S(2)}, u32[]{:S(2)}) async-start(bf16[128,1,32]{2,1,0:T(2,128)(2,1)} %all_to_all.32), calls=%async_computation.2 | async-start | bytes 131072 | tf_op jit(solution)/shard_map/all_to_all | solution.py:78
  37.4 8.1 %scatter_custom_fusion.1 = s32[4096]{0:T(1024)S(1)} fusion(s32[2048]{0:T(1024)S(1)} %bitcast.44, s32[2048]{0:T(1024)S(1)} %multiply_add_fusion, s32[]{:T(128)} %constant.12.clone.1), kind=kCustom, calls=%fused_computation.36 | custom fusion | bytes 16388 | tf_op jit(solution)/shard_map/scatter | solution.py:69
  45.5 0.7 all_to_all.25
  46.2 0.7 all-to-all-done.2
  46.9 9.1 %all-to-all-start.1 = ((s32[128,1,32]{2,1,0:T(1,128)}), s32[128,1,32]{2,1,0:T(1,128)S(1)}, u32[]{:S(2)}, u32[]{:S(2)}) async-start(s32[128,1,32]{2,1,0:T(1,128)} %bitcast.8), calls=%async_computation.1 | async-start | bytes 131072 | tf_op jit(solution)/shard_map/all_to_all | solution.py:81
  55.9 7.2 %scatter_custom_fusion = bf16[4096,128]{1,0:T(8,128)(2,1)} fusion(s32[2048]{0:T(1024)S(1)} %bitcast.45, bf16[2048,128]{1,0:T(8,128)(2,1)} %param.15, bf16[]{:T(256)} %constant.10.clone.1), kind=kCustom, calls=%fused_computation.26 | custom fusion | bytes 1049088 | tf_op jit(solution)/shard_map/scatter | solution.py:67
  63.1 2.3 all-to-all-done.1
  65.4 7.4 %all-to-all-start = ((bf16[128,32,128]{2,1,0:T(8,128)(2,1)}), bf16[128,32,128]{2,1,0:T(8,128)(2,1)S(1)}, u32[]{:S(2)}, u32[]{:S(2)}) async-start(bf16[128,32,128]{2,1,0:T(8,128)(2,1)} %bitcast.7), calls=%async_computation | async-start | bytes 2097152 | tf_op jit(solution)/shard_map/all_to_all | solution.py:71
  72.9 0.2 all-gather.2.cloned.1.call-start
  73.1 0.2 convert_reduce_fusion
  73.3 0.1 reshape.115
  73.4 0.5 broadcast.93
  73.9 0.8 reduce.11
  74.7 0.1 reshape.111
  74.8 17.1 %all-to-all-done = bf16[128,32,128]{2,1,0:T(8,128)(2,1)S(1)} async-done(((bf16[128,32,128]{2,1,0:T(8,128)(2,1)}), bf16[128,32,128]{2,1,0:T(8,128)(2,1)S(1)}, u32[]{:S(2)}, u32[]{:S(2)}) %all-to-all-start) | async-done | bytes 1048608 | tf_op jit(solution)/shard_map/all_to_all | solution.py:71
  91.9 2.0 bitcast_multiply_fusion
  93.9 23.6 %scatter_custom_fusion.3 = f32[1152,128]{1,0:T(8,128)S(1)} fusion(s32[4096]{0:T(1024)S(1)} %bitcast.41, f32[4096,128]{1,0:T(8,128)} %bitcast_multiply_fusion, f32[]{:T(128)} %constant.9.clone.1), kind=kCustom, calls=%fused_computation.28 | custom fusion | flops 524288 | bytes 590336 | tf_op jit(solution)/shard_map/scatter-add | solution.py:89
  117.5 0.4 convert_element_type.64
  117.9 0.2 copy.24
  118.1 0.3 broadcast_in_dim.11
  118.4 33.0 %all_to_all.38 = bf16[8,1152,128]{2,1,0:T(8,128)(2,1)S(1)} all-to-all(bf16[8,1152,128]{2,1,0:T(8,128)(2,1)S(1)} %broadcast_in_dim.11), channel_id=1, replica_groups=mesh['cell_0'=4,'cell_1'=2,'tm_0'=4,'tm_1'=4] {'cell_0','cell_1'}, dimensions={0} | all-to-all | bytes 4718592 | tf_op jit(solution)/shard_map/all_to_all | solution.py:21
  151.4 11.7 %fusion.1 = bf16[1152,128]{0,1:T(8,128)(2,1)} fusion(bf16[9216,128]{1,0:T(8,128)(2,1)S(1)} %bitcast.36, bf16[1152,9216]{1,0:T(8,128)(2,1)} %param.20), kind=kOutput, calls=%fused_computation.9 | convolution fusion | flops 2718056448 | bytes 23887872 | tf_op jit(solution)/shard_map/dot_general | solution.py:91
  163.1 49.9 %all-gather.2.cloned.1.call-done = bf16[1152,2048]{0,1:T(8,128)(2,1)} async-done(((bf16[1152,128]{0,1:T(8,128)(2,1)}), bf16[1152,2048]{0,1:T(8,128)(2,1)}) %all-gather.2.cloned.1.call-update) | async-done | bytes 4718608 | tf_op jit(solution)/shard_map/all_gather | solution.py:96
  213.0 3.8 %fusion = bf16[128,1152]{0,1:T(8,128)(2,1)S(1)} fusion(bf16[1152,2048]{0,1:T(8,128)(2,1)} %all-gather.2.cloned.1.call-done, bf16[128,2048]{1,0:T(8,128)(2,1)S(1)} %copy-done), kind=kOutput, calls=%fused_computation.8 | convolution fusion | flops 604127232 | bytes 5537792 | tf_op jit(solution)/shard_map/dot_general | solution.py:94
  216.8 0.2 copy.25
  217.0 0.3 reshape.113
  217.4 12.1 %gather_fusion = bf16[4096,128]{1,0:T(8,128)(2,1)S(1)} fusion(bf16[1152,128]{1,0:T(8,128)(2,1)S(1)} %reshape.113, s32[4096]{0:T(1024)S(1)} %broadcast_clamp_fusion), kind=kCustom, calls=%fused_computation | custom fusion | bytes 2113536 | tf_op jit(solution)/shard_map/gather | solution.py:101
  229.5 1.3 fusion.2
  230.8 8.4 %all-to-all-start.4 = ((f32[128,1,32]{2,1,0:T(1,128)}), f32[128,1,32]{2,1,0:T(1,128)S(1)}, u32[]{:S(2)}, u32[]{:S(2)}) async-start(f32[128,1,32]{2,1,0:T(1,128)} %bitcast.18), calls=%async_computation.4 | async-start | bytes 131072 | tf_op jit(solution)/shard_map/all_to_all | solution.py:102
  239.2 9.5 %all-to-all-done.4 = f32[128,1,32]{2,1,0:T(1,128)S(1)} async-done(((f32[128,1,32]{2,1,0:T(1,128)}), f32[128,1,32]{2,1,0:T(1,128)S(1)}, u32[]{:S(2)}, u32[]{:S(2)}) %all-to-all-start.4) | async-done | bytes 16416 | tf_op jit(solution)/shard_map/all_to_all | solution.py:102
  248.7 0.5 broadcast.94
  249.2 0.8 reduce.12
  250.1 11.8 %gather_fusion.1 = f32[2048]{0:T(1024)S(1)} fusion(f32[4096]{0:T(1024)S(1)} %reshape.114, s32[2048]{0:T(1024)S(1)} %broadcast_clamp_fusion.1), kind=kCustom, calls=%fused_computation.1 | custom fusion | bytes 24576 | tf_op jit(solution)/shard_map/gather | solution.py:105
  261.9 0.8 fusion.3
  262.7 0.6 multiply_reduce_fusion
  263.3 9.3 %all-reduce.2 = (f32[]{:T(128)}, f32[]{:T(128)}, f32[]{:T(128)}, f32[]{:T(128)}) all-reduce(f32[]{:T(128)} %get-tuple-element.5, f32[]{:T(128)} %get-tuple-element.6, f32[]{:T(128)} %get-tuple-element.4, f32[]{:T(128)} %get-tuple-element.3), channel_id=1, replica_groups=mesh['cell_0'=4,'cell_1'=2,'tm_0'=4,'tm_1'=4] {'cell_0'}, use_global_device_ids=true, to_apply=%region_1.2 | all-reduce | flops 4 | bytes 32 | tf_op jit(solution)/shard_map/psum | solution.py:31
  272.6 3.1 %all-reduce.3 = (f32[]{:T(128)}, f32[]{:T(128)}, f32[]{:T(128)}, f32[]{:T(128)}) all-reduce(f32[]{:T(128)} %get-tuple-element.15, f32[]{:T(128)} %get-tuple-element.16, f32[]{:T(128)} %get-tuple-element.17, f32[]{:T(128)} %get-tuple-element.18), channel_id=1, replica_groups=mesh['cell_0'=4,'cell_1'=2,'tm_0'=4,'tm_1'=4] {'cell_1'}, use_global_device_ids=true, to_apply=%region_2.3 | all-reduce | flops 4 | bytes 32 | tf_op jit(solution)/shard_map/psum | solution.py:31
  275.7 9.1 %all-reduce.1 = (f32[]{:T(128)}, f32[]{:T(128)}, f32[]{:T(128)}, f32[]{:T(128)}) all-reduce(f32[]{:T(128)} %get-tuple-element.19, f32[]{:T(128)} %get-tuple-element.20, f32[]{:T(128)} %get-tuple-element.21, f32[]{:T(128)} %get-tuple-element.22), channel_id=1, replica_groups=mesh['cell_0'=4,'cell_1'=2,'tm_0'=4,'tm_1'=4] {'tm_0'}, use_global_device_ids=true, to_apply=%region_3.4 | all-reduce | flops 4 | bytes 32 | tf_op jit(solution)/shard_map/psum | solution.py:31
  284.8 9.7 %all-reduce = (f32[]{:T(128)}, f32[]{:T(128)}, f32[]{:T(128)}, f32[]{:T(128)}) all-reduce(f32[]{:T(128)} %get-tuple-element.11, f32[]{:T(128)} %get-tuple-element.12, f32[]{:T(128)} %get-tuple-element.13, f32[]{:T(128)} %get-tuple-element.14), channel_id=1, replica_groups=mesh['cell_0'=4,'cell_1'=2,'tm_0'=4,'tm_1'=4] {'tm_1'}, use_global_device_ids=true, to_apply=%region_4.5 | all-reduce | flops 4 | bytes 32 | tf_op jit(solution)/shard_map/psum | solution.py:31
  298.3 0.6 multiply_add_fusion.1
  (31 shorter events, 0.4 us)
Async XLA Ops:
  7.2 205.9 %copy-start = (bf16[128,2048]{1,0:T(8,128)(2,1)S(1)}, bf16[128,2048]{1,0:T(8,128)(2,1)}, u32[]{:S(2)}) copy-start(bf16[128,2048]{1,0:T(8,128)(2,1)} %param.21) | copy-start | bytes 1572868
  8.4 0.7 copy-start.1
  8.5 1.3 copy-start.4
  8.5 1.3 copy-start.8
  8.5 28.8 %copy-start.2 = (s32[2048]{0:T(1024)S(1)}, s32[2048]{0:T(1024)}, u32[]{:S(2)}) copy-start(s32[2048]{0:T(1024)} %param.17) | copy-start | bytes 24580
  8.6 28.8 %copy-start.3 = (s32[2048]{0:T(1024)S(1)}, s32[2048]{0:T(1024)}, u32[]{:S(2)}) copy-start(s32[2048]{0:T(1024)} %param.18) | copy-start | bytes 24580
  26.2 20.7 %all-to-all-start.2 = ((bf16[128,1,32]{2,1,0:T(2,128)(2,1)}), bf16[128,1,32]{2,1,0:T(2,128)(2,1)S(1)}, u32[]{:S(2)}, u32[]{:S(2)}) async-start(bf16[128,1,32]{2,1,0:T(2,128)(2,1)} %all_to_all.32), calls=%async_computation.2 | async-start | bytes 131072 | tf_op jit(solution)/shard_map/all_to_all | solution.py:78
  46.9 18.6 %all-to-all-start.1 = ((s32[128,1,32]{2,1,0:T(1,128)}), s32[128,1,32]{2,1,0:T(1,128)S(1)}, u32[]{:S(2)}, u32[]{:S(2)}) async-start(s32[128,1,32]{2,1,0:T(1,128)} %bitcast.8), calls=%async_computation.1 | async-start | bytes 131072 | tf_op jit(solution)/shard_map/all_to_all | solution.py:81
  65.4 26.5 %all-to-all-start = ((bf16[128,32,128]{2,1,0:T(8,128)(2,1)}), bf16[128,32,128]{2,1,0:T(8,128)(2,1)S(1)}, u32[]{:S(2)}, u32[]{:S(2)}) async-start(bf16[128,32,128]{2,1,0:T(8,128)(2,1)} %bitcast.7), calls=%async_computation | async-start | bytes 2097152 | tf_op jit(solution)/shard_map/all_to_all | solution.py:71
  72.9 140.2 %all-gather.2.cloned.1.call-start = ((), (), s32[]{:S(2)}) async-start(), calls=%async_computation.5 | async-start | bytes 5013504 | tf_op jit(solution)/shard_map/all_gather | solution.py:96
  230.8 17.9 %all-to-all-start.4 = ((f32[128,1,32]{2,1,0:T(1,128)}), f32[128,1,32]{2,1,0:T(1,128)S(1)}, u32[]{:S(2)}, u32[]{:S(2)}) async-start(f32[128,1,32]{2,1,0:T(1,128)} %bitcast.18), calls=%async_computation.4 | async-start | bytes 131072 | tf_op jit(solution)/shard_map/all_to_all | solution.py:102
  250.1 12.6 %copy-start.5 = (f32[256]{0:T(256)S(1)}, f32[256]{0:T(256)}, u32[]{:S(2)}) copy-start(f32[256]{0:T(256)} %param.12) | copy-start | bytes 3076
  250.1 12.6 %copy-start.6 = (f32[256]{0:T(256)S(1)}, f32[256]{0:T(256)}, u32[]{:S(2)}) copy-start(f32[256]{0:T(256)} %param.14) | copy-start | bytes 3076
  250.1 48.3 %copy-start.7 = (f32[256]{0:T(256)S(1)}, f32[256]{0:T(256)}, u32[]{:S(2)}) copy-start(f32[256]{0:T(256)} %param.11) | copy-start | bytes 3076
Sparse Core Ops, SparseCore 0:
  163.2 49.7 all-gather.1
where the time goes:
time: 306 us
  waiting for transfers between devices  79.5 us (26%)
  blocking collectives  64.2 us (21%)
  local copies, waits for them, and re-layouts  59.3 us (19%)
  starting transfers between devices  36.3 us (12%)
  other arithmetic  31 us (10%)
  between operations  18.3 us (6%)
  matrix products  17.3 us (6%)
    all_gather x1, waiting for transfers between devices, local(): lax.all_gather(mixed_cells, TM, axis=1, tiled=True)  49.9 us
    all_to_all x1, blocking collectives, from_everyone(): lax.all_to_all(jnp.broadcast_to(value[None], (peers, *value.shape)), axis...  33 us
    psum x4, blocking collectives, over_axes(): return functools.reduce(lax.psum, axes, value)  31.2 us
    scatter-add x1, other arithmetic, local(): flux_time = flux_time.at[got_place].add(got_dir[:, None] * got_values)  23.6 us
    all_to_all x1, waiting for transfers between devices, local(): lax.all_to_all(send_values.reshape(devices, capacity, block_len), CELL_TM...  17.1 us
    scatter x1, local copies, waits for them, and re-layouts, local(): jnp.zeros((slot_total,), jnp.bfloat16).at[slot_index].set(dir_tile)  14.6 us
    gather x1, local copies, waits for them, and re-layouts, local(): smoothed[got_place].astype(jnp.float32)  12.1 us
    gather x1, local copies, waits for them, and re-layouts, local(): tile_dots = returned.reshape(slot_total)[slot_index]  11.8 us
  transfers between devices with their start and end apart: 5, of which 5 were waited for; matrix products, arithmetic and copies ran while one was open for 6% of the time, Pallas kernels for 0%

commit v1 on v0

--- a/solution.py
+++ b/solution.py
@@ -8,6 +8,13 @@
 CELL = ("cell_0", "cell_1")
 TM = ("tm_0", "tm_1")
 CELL_TM = ("cell_0", "cell_1", "tm_0", "tm_1")
+
+
+def gather_over(value, name, dim):
+    size = lax.axis_size(name)
+    shards = jnp.stack([value for _ in range(size)])
+    shards = lax.all_to_all(shards, name, split_axis=0, concat_axis=0)
+    return jnp.concatenate(shards, axis=dim)
 
 
 def laid_out(pieces, dim):
@@ -93,7 +100,7 @@
     ).astype(jnp.bfloat16)
     smoothed = lax.dot_general(
         time_cov,
-        lax.all_gather(mixed_cells, TM, axis=1, tiled=True),
+        gather_over(mixed_cells, TM, 1),
         (((1,), (1,)), ((), ())),
         preferred_element_type=jnp.float32,
     )

time: 306 us -> 319 us (1.042)
  waiting for transfers between devices: 79.5 us -> 100 us
  between operations: 18.3 us -> 4.88 us
    all_to_all x0 -> x1, waiting for transfers between devices: none -> 70.6 us  [gather_over(): shards = lax.all_to_all(shards, name, split_axis=0, concat_axis=0)]
    all_gather x1 -> x0, waiting for transfers between devices: 49.9 us -> none  [local(): lax.all_gather(mixed_cells, TM, axis=1, tiled=True)]
    all_to_all x0 -> x1, starting transfers between devices: none -> 4.56 us  [gather_over(): shards = lax.all_to_all(shards, name, split_axis=0, concat_axis=0)]
  transfers between devices with their start and end apart: 5 -> 5, of which waited for: 5 -> 5; matrix products, arithmetic and copies ran while one was open for 6% -> 5% of each run, Pallas kernels for 0% -> 0%
where the time goes in v1:
time: 319 us; the launch traced here: 318 us
  waiting for transfers between devices  100 us (31%)
  blocking collectives  64.2 us (20%)
  local copies, waits for them, and re-layouts  62.1 us (19%)
  starting transfers between devices  38.9 us (12%)
  other arithmetic  30.9 us (10%)
  matrix products  16.8 us (5%)
  between operations  4.88 us (2%)
    all_to_all x1, waiting for transfers between devices, gather_over(): shards = lax.all_to_all(shards, name, split_axis=0, concat_axis=0)  70.6 us
    all_to_all x1, blocking collectives, from_everyone(): lax.all_to_all(jnp.broadcast_to(value[None], (peers, *value.shape)), axis...  33 us
    psum x4, blocking collectives, over_axes(): return functools.reduce(lax.psum, axes, value)  31.2 us
    scatter-add x1, other arithmetic, local(): flux_time = flux_time.at[got_place].add(got_dir[:, None] * got_values)  23.6 us
    all_to_all x1, waiting for transfers between devices, local(): lax.all_to_all(send_values.reshape(devices, capacity, block_len), CELL_TM...  17.1 us
    scatter x1, local copies, waits for them, and re-layouts, local(): jnp.zeros((slot_total,), jnp.bfloat16).at[slot_index].set(dir_tile)  14.6 us
    gather x1, local copies, waits for them, and re-layouts, local(): smoothed[got_place].astype(jnp.float32)  12.1 us
    gather x1, local copies, waits for them, and re-layouts, local(): tile_dots = returned.reshape(slot_total)[slot_index]  11.8 us
  transfers between devices with their start and end apart: 5, of which 5 were waited for; matrix products, arithmetic and copies ran while one was open for 5% of the time, Pallas kernels for 0%

profile of v1, /device:TPU:0, one launch (start us, length us, event | category | flops | bytes accessed | tf_op | source)
XLA Modules:
  0.0 318.0 jit_solution(14926898839526370508)
XLA Ops:
  0.6 0.9 copy.21
  1.5 0.3 fusion.8
  2.0 0.3 copy.22
  2.4 0.2 copy-done.1
  2.6 0.6 fusion.5
  3.3 1.0 fusion.4
  4.3 14.6 %scatter_custom_fusion.2 = bf16[4096]{0:T(1024)(128)(2,1)S(1)} fusion(s32[2048]{0:T(1024)S(1)} %bitcast.46, bf16[2048]{0:T(1024)(128)(2,1)S(1)} %convert_element_type.58, bf16[]{:T(256)} %constant.10.clone.1), kind=kCustom, calls=%fused_computation.39 | custom fusion | bytes 8194 | tf_op jit(solution)/shard_map/scatter | solution.py:75
  18.9 0.7 all_to_all.36
  19.6 11.2 %all-to-all-start.2 = ((bf16[128,1,32]{2,1,0:T(2,128)(2,1)}), bf16[128,1,32]{2,1,0:T(2,128)(2,1)S(1)}, u32[]{:S(2)}, u32[]{:S(2)}) async-start(bf16[128,1,32]{2,1,0:T(2,128)(2,1)} %all_to_all.36), calls=%async_computation.2 | async-start | bytes 131072 | tf_op jit(solution)/shard_map/all_to_all | solution.py:85
  30.9 8.1 %scatter_custom_fusion.1 = s32[4096]{0:T(1024)S(1)} fusion(s32[2048]{0:T(1024)S(1)} %bitcast.47, s32[2048]{0:T(1024)S(1)} %multiply_add_fusion, s32[]{:T(128)} %constant.12.clone.1), kind=kCustom, calls=%fused_computation.36 | custom fusion | bytes 16388 | tf_op jit(solution)/shard_map/scatter | solution.py:76
  38.9 0.7 all_to_all.28
  39.6 0.7 all-to-all-done.2
  40.3 9.1 %all-to-all-start.1 = ((s32[128,1,32]{2,1,0:T(1,128)}), s32[128,1,32]{2,1,0:T(1,128)S(1)}, u32[]{:S(2)}, u32[]{:S(2)}) async-start(s32[128,1,32]{2,1,0:T(1,128)} %bitcast.8), calls=%async_computation.1 | async-start | bytes 131072 | tf_op jit(solution)/shard_map/all_to_all | solution.py:88
  49.4 7.2 %scatter_custom_fusion = bf16[4096,128]{1,0:T(8,128)(2,1)} fusion(s32[2048]{0:T(1024)S(1)} %bitcast.48, bf16[2048,128]{1,0:T(8,128)(2,1)} %param.15, bf16[]{:T(256)} %constant.10.clone.1), kind=kCustom, calls=%fused_computation.26 | custom fusion | bytes 1049088 | tf_op jit(solution)/shard_map/scatter | solution.py:74
  56.6 2.3 all-to-all-done.1
  58.9 7.6 %all-to-all-start = ((bf16[128,32,128]{2,1,0:T(8,128)(2,1)}), bf16[128,32,128]{2,1,0:T(8,128)(2,1)S(1)}, u32[]{:S(2)}, u32[]{:S(2)}) async-start(bf16[128,32,128]{2,1,0:T(8,128)(2,1)} %bitcast.7), calls=%async_computation | async-start | bytes 2097152 | tf_op jit(solution)/shard_map/all_to_all | solution.py:78
  66.5 0.2 convert_reduce_fusion
  66.8 0.5 broadcast.95
  67.3 0.8 reduce.11
  68.1 0.1 reshape.119
  68.2 17.1 %all-to-all-done = bf16[128,32,128]{2,1,0:T(8,128)(2,1)S(1)} async-done(((bf16[128,32,128]{2,1,0:T(8,128)(2,1)}), bf16[128,32,128]{2,1,0:T(8,128)(2,1)S(1)}, u32[]{:S(2)}, u32[]{:S(2)}) %all-to-all-start) | async-done | bytes 1048608 | tf_op jit(solution)/shard_map/all_to_all | solution.py:78
  85.4 2.0 bitcast_multiply_fusion
  87.3 23.6 %scatter_custom_fusion.3 = f32[1152,128]{1,0:T(8,128)S(1)} fusion(s32[4096]{0:T(1024)S(1)} %bitcast.44, f32[4096,128]{1,0:T(8,128)} %bitcast_multiply_fusion, f32[]{:T(128)} %constant.9.clone.1), kind=kCustom, calls=%fused_computation.28 | custom fusion | flops 524288 | bytes 590336 | tf_op jit(solution)/shard_map/scatter-add | solution.py:96
  110.9 0.4 convert_element_type.64
  111.3 0.2 copy.25
  111.5 0.3 broadcast_in_dim.11
  111.8 33.0 %all_to_all.43 = bf16[8,1152,128]{2,1,0:T(8,128)(2,1)S(1)} all-to-all(bf16[8,1152,128]{2,1,0:T(8,128)(2,1)S(1)} %broadcast_in_dim.11), channel_id=1, replica_groups=mesh['cell_0'=4,'cell_1'=2,'tm_0'=4,'tm_1'=4] {'cell_0','cell_1'}, dimensions={0} | all-to-all | bytes 4718592 | tf_op jit(solution)/shard_map/all_to_all | solution.py:28
  144.9 11.2 %fusion.1 = bf16[1152,128]{0,1:T(8,128)(2,1)S(1)} fusion(bf16[9216,128]{1,0:T(8,128)(2,1)S(1)} %bitcast.39, bf16[1152,9216]{1,0:T(8,128)(2,1)} %param.20), kind=kOutput, calls=%fused_computation.9 | convolution fusion | flops 2718056448 | bytes 23887872 | tf_op jit(solution)/shard_map/dot_general | solution.py:98
  156.0 2.8 stack.2
  158.8 4.6 %all-to-all-start.4 = ((bf16[16,1152,128]{1,2,0:T(8,128)(2,1)}), bf16[16,1152,128]{1,2,0:T(8,128)(2,1)}, u32[]{:S(2)}, u32[]{:S(2)}) async-start(bf16[16,1152,128]{1,2,0:T(8,128)(2,1)} %stack.2), calls=%async_computation.4 | async-start | bytes 9437184 | tf_op jit(solution)/shard_map/all_to_all | solution.py:16
  163.4 70.6 %all-to-all-done.4 = bf16[16,1152,128]{1,2,0:T(8,128)(2,1)} async-done(((bf16[16,1152,128]{1,2,0:T(8,128)(2,1)}), bf16[16,1152,128]{1,2,0:T(8,128)(2,1)}, u32[]{:S(2)}, u32[]{:S(2)}) %all-to-all-start.4) | async-done | bytes 4718624 | tf_op jit(solution)/shard_map/all_to_all | solution.py:16
  234.0 3.8 %fusion = bf16[128,1152]{0,1:T(8,128)(2,1)S(1)} fusion(bf16[1152,2048]{0,1:T(8,128)(2,1)} %bitcast.17, bf16[128,2048]{1,0:T(8,128)(2,1)S(1)} %copy-done), kind=kOutput, calls=%fused_computation.8 | convolution fusion | flops 604127232 | bytes 5537792 | tf_op jit(solution)/shard_map/dot_general | solution.py:101
  237.8 0.2 copy.26
  238.0 0.3 reshape.123
  238.3 12.1 %gather_fusion = bf16[4096,128]{1,0:T(8,128)(2,1)S(1)} fusion(bf16[1152,128]{1,0:T(8,128)(2,1)S(1)} %reshape.123, s32[4096]{0:T(1024)S(1)} %broadcast_clamp_fusion), kind=kCustom, calls=%fused_computation | custom fusion | bytes 2113536 | tf_op jit(solution)/shard_map/gather | solution.py:108
  250.5 1.2 fusion.2
  251.7 6.5 %all-to-all-start.5 = ((f32[128,1,32]{2,1,0:T(1,128)}), f32[128,1,32]{2,1,0:T(1,128)S(1)}, u32[]{:S(2)}, u32[]{:S(2)}) async-start(f32[128,1,32]{2,1,0:T(1,128)} %bitcast.20), calls=%async_computation.5 | async-start | bytes 131072 | tf_op jit(solution)/shard_map/all_to_all | solution.py:109
  258.2 9.5 %all-to-all-done.5 = f32[128,1,32]{2,1,0:T(1,128)S(1)} async-done(((f32[128,1,32]{2,1,0:T(1,128)}), f32[128,1,32]{2,1,0:T(1,128)S(1)}, u32[]{:S(2)}, u32[]{:S(2)}) %all-to-all-start.5) | async-done | bytes 16416 | tf_op jit(solution)/shard_map/all_to_all | solution.py:109
  267.7 0.5 broadcast.96
  268.2 0.8 reduce.12
  269.2 11.8 %gather_fusion.1 = f32[2048]{0:T(1024)S(1)} fusion(f32[4096]{0:T(1024)S(1)} %reshape.124, s32[2048]{0:T(1024)S(1)} %broadcast_clamp_fusion.1), kind=kCustom, calls=%fused_computation.1 | custom fusion | bytes 24576 | tf_op jit(solution)/shard_map/gather | solution.py:112
  281.0 0.8 fusion.3
  281.8 0.6 multiply_reduce_fusion
  282.4 9.3 %all-reduce.2 = (f32[]{:T(128)}, f32[]{:T(128)}, f32[]{:T(128)}, f32[]{:T(128)}) all-reduce(f32[]{:T(128)} %get-tuple-element.5, f32[]{:T(128)} %get-tuple-element.6, f32[]{:T(128)} %get-tuple-element.4, f32[]{:T(128)} %get-tuple-element.3), channel_id=1, replica_groups=mesh['cell_0'=4,'cell_1'=2,'tm_0'=4,'tm_1'=4] {'cell_0'}, use_global_device_ids=true, to_apply=%region_1.2 | all-reduce | flops 4 | bytes 32 | tf_op jit(solution)/shard_map/psum | solution.py:38
  291.7 3.1 all-reduce.3
  294.8 9.1 %all-reduce.1 = (f32[]{:T(128)}, f32[]{:T(128)}, f32[]{:T(128)}, f32[]{:T(128)}) all-reduce(f32[]{:T(128)} %get-tuple-element.19, f32[]{:T(128)} %get-tuple-element.20, f32[]{:T(128)} %get-tuple-element.21, f32[]{:T(128)} %get-tuple-element.22), channel_id=1, replica_groups=mesh['cell_0'=4,'cell_1'=2,'tm_0'=4,'tm_1'=4] {'tm_0'}, use_global_device_ids=true, to_apply=%region_3.4 | all-reduce | flops 4 | bytes 32 | tf_op jit(solution)/shard_map/psum | solution.py:38
  303.9 9.7 %all-reduce = (f32[]{:T(128)}, f32[]{:T(128)}, f32[]{:T(128)}, f32[]{:T(128)}) all-reduce(f32[]{:T(128)} %get-tuple-element.11, f32[]{:T(128)} %get-tuple-element.12, f32[]{:T(128)} %get-tuple-element.13, f32[]{:T(128)} %get-tuple-element.14), channel_id=1, replica_groups=mesh['cell_0'=4,'cell_1'=2,'tm_0'=4,'tm_1'=4] {'tm_1'}, use_global_device_ids=true, to_apply=%region_4.5 | all-reduce | flops 4 | bytes 32 | tf_op jit(solution)/shard_map/psum | solution.py:38
  317.4 0.6 multiply_add_fusion.1
  (31 shorter events, 0.4 us)
Async XLA Ops:
  0.6 233.4 %copy-start = (bf16[128,2048]{1,0:T(8,128)(2,1)S(1)}, bf16[128,2048]{1,0:T(8,128)(2,1)}, u32[]{:S(2)}) copy-start(bf16[128,2048]{1,0:T(8,128)(2,1)} %param.21) | copy-start | bytes 1572868
  1.9 0.7 copy-start.1
  2.0 1.3 copy-start.4
  2.0 1.3 copy-start.8
  2.0 28.8 %copy-start.2 = (s32[2048]{0:T(1024)S(1)}, s32[2048]{0:T(1024)}, u32[]{:S(2)}) copy-start(s32[2048]{0:T(1024)} %param.17) | copy-start | bytes 24580
  2.0 28.8 %copy-start.3 = (s32[2048]{0:T(1024)S(1)}, s32[2048]{0:T(1024)}, u32[]{:S(2)}) copy-start(s32[2048]{0:T(1024)} %param.18) | copy-start | bytes 24580
  19.6 20.7 %all-to-all-start.2 = ((bf16[128,1,32]{2,1,0:T(2,128)(2,1)}), bf16[128,1,32]{2,1,0:T(2,128)(2,1)S(1)}, u32[]{:S(2)}, u32[]{:S(2)}) async-start(bf16[128,1,32]{2,1,0:T(2,128)(2,1)} %all_to_all.36), calls=%async_computation.2 | async-start | bytes 131072 | tf_op jit(solution)/shard_map/all_to_all | solution.py:85
  40.3 18.6 %all-to-all-start.1 = ((s32[128,1,32]{2,1,0:T(1,128)}), s32[128,1,32]{2,1,0:T(1,128)S(1)}, u32[]{:S(2)}, u32[]{:S(2)}) async-start(s32[128,1,32]{2,1,0:T(1,128)} %bitcast.8), calls=%async_computation.1 | async-start | bytes 131072 | tf_op jit(solution)/shard_map/all_to_all | solution.py:88
  58.9 26.5 %all-to-all-start = ((bf16[128,32,128]{2,1,0:T(8,128)(2,1)}), bf16[128,32,128]{2,1,0:T(8,128)(2,1)S(1)}, u32[]{:S(2)}, u32[]{:S(2)}) async-start(bf16[128,32,128]{2,1,0:T(8,128)(2,1)} %bitcast.7), calls=%async_computation | async-start | bytes 2097152 | tf_op jit(solution)/shard_map/all_to_all | solution.py:78
  158.8 75.2 %all-to-all-start.4 = ((bf16[16,1152,128]{1,2,0:T(8,128)(2,1)}), bf16[16,1152,128]{1,2,0:T(8,128)(2,1)}, u32[]{:S(2)}, u32[]{:S(2)}) async-start(bf16[16,1152,128]{1,2,0:T(8,128)(2,1)} %stack.2), calls=%async_computation.4 | async-start | bytes 9437184 | tf_op jit(solution)/shard_map/all_to_all | solution.py:16
  251.7 16.0 %all-to-all-start.5 = ((f32[128,1,32]{2,1,0:T(1,128)}), f32[128,1,32]{2,1,0:T(1,128)S(1)}, u32[]{:S(2)}, u32[]{:S(2)}) async-start(f32[128,1,32]{2,1,0:T(1,128)} %bitcast.20), calls=%async_computation.5 | async-start | bytes 131072 | tf_op jit(solution)/shard_map/all_to_all | solution.py:109
  269.1 12.6 %copy-start.5 = (f32[256]{0:T(256)S(1)}, f32[256]{0:T(256)}, u32[]{:S(2)}) copy-start(f32[256]{0:T(256)} %param.12) | copy-start | bytes 3076
  269.1 12.6 %copy-start.6 = (f32[256]{0:T(256)S(1)}, f32[256]{0:T(256)}, u32[]{:S(2)}) copy-start(f32[256]{0:T(256)} %param.14) | copy-start | bytes 3076
  269.2 48.3 %copy-start.7 = (f32[256]{0:T(256)S(1)}, f32[256]{0:T(256)}, u32[]{:S(2)}) copy-start(f32[256]{0:T(256)} %param.11) | copy-start | bytes 3076
